TPU v7x, 32 devices: a whole 2x2x4 slice. The times are simulated.
32 devices in a mesh: lang: 2 (over y), clu: 16 (over z, x, core).
Axes of the slice: x: 2, y: 2, z: 4, core: 2. Of those that a mesh axis runs over, the one named last changes fastest.
Arguments:
- embeddings: bfloat16 [8192, 1024], P(('lang', 'clu')), parts along dimension 0, may hold values from -6 to 6
- assignment: int32 [8192, 1], P(('lang', 'clu')), parts along dimension 0, may hold values from 0 to 31; in each aligned block of 256 rows (0 to 255, 256 to 511, ...) at most 16 rows name the same one
Outputs:
- best_similarity: float32 [8192], P(('lang', 'clu')), parts along dimension 0
There are 2 independent parts, one for each index of `lang`. A program takes and returns all parts, laid end to end along the dimension named above; each array names one. Nothing has to cross between parts.
Inputs may be any that keep to these rules, and one draw needn't show every extreme that they name: `assignment`: in each aligned block of 256 rows (the rows of one device) no cluster is named by more than 16 rows; every cluster is named by some row.
All inputs are finite; a program needn't handle non-finite values.
Results may differ from a plain program's by a relative error of at most 0.0016.
Values may be sent and summed in bfloat16 or wider, within the bound.
A program may use at most 64 MiB of HBM per device.

v0:
```python
import functools

import jax
import jax.numpy as jnp
from jax import lax
from jax.experimental import pallas as pl
from jax.experimental.pallas import tpu as pltpu
from jax.sharding import PartitionSpec as P

CLU_DEV = 2
LANES = 128
EPS = 1e-06
DEAD = 4.0


def normalize(embeddings):
    values = embeddings.astype(jnp.float32)
    scale = lax.rsqrt(jnp.sum(values * values, axis=-1, keepdims=True) + EPS)
    return (values * scale).astype(jnp.bfloat16)


def exchange_kernel(
    groups, most, emb_ref, cluster_ref, out_ref,
    unit, outgoing, arrived, best, returned,
    load_sem, send_sem, recv_sem, back_send_sem, back_recv_sem, ready,
):
    count, width = unit.shape
    block = CLU_DEV * most
    total = groups * block
    batch = LANES // block
    me = lax.axis_index("clu")
    chunks = 4
    step = count // chunks

    def load(c):
        rows = pl.ds(c * step, step)
        return pltpu.make_async_copy(emb_ref.at[rows], unit.at[rows], load_sem.at[c])

    for c in range(chunks):
        load(c).start()

    barrier = pltpu.get_barrier_semaphore()
    bits = groups.bit_length() - 1
    for b in range(bits):
        pl.semaphore_signal(
            barrier, inc=1, device_id={"clu": me ^ (1 << b)},
            device_id_type=pl.DeviceIdType.MESH,
        )

    def tell(stage):
        for b in range(bits):
            pl.semaphore_signal(
                ready.at[stage, b], inc=1, device_id={"clu": me ^ (1 << b)},
                device_id_type=pl.DeviceIdType.MESH,
            )

    def hear(stage):
        for b in range(bits):
            pl.semaphore_wait(ready.at[stage, b], 1)

    def slot_of(cluster, rank):
        peer = (cluster // CLU_DEV) ^ me
        return peer * block + (cluster % CLU_DEV) * most + rank

    cluster_row = cluster_ref[...]
    row_id = lax.broadcasted_iota(jnp.int32, (count, count), 0)
    col_id = lax.broadcasted_iota(jnp.int32, (count, count), 1)
    spread = jnp.broadcast_to(cluster_row, (count, count))
    cluster_col = jnp.sum(jnp.where(row_id == col_id, spread, 0), axis=1, keepdims=True)
    same = cluster_col == spread
    rank_row = jnp.sum(jnp.where(same & (row_id < col_id), 1, 0), axis=0, keepdims=True)
    slot_row = jnp.broadcast_to(slot_of(cluster_row, rank_row), (LANES, count))

    for c in range(chunks):
        load(c).wait()
        rows = pl.ds(c * step, step)
        unit[rows, :] = normalize(unit[rows, :])

    def send(k):
        rows = pl.ds(pl.multiple_of(k * block, block), block)
        return pltpu.make_async_remote_copy(
            src_ref=outgoing.at[rows],
            dst_ref=arrived.at[rows],
            send_sem=send_sem.at[k],
            recv_sem=recv_sem.at[k],
            device_id={"clu": me ^ k},
            device_id_type=pl.DeviceIdType.MESH,
        )

    first = lax.broadcasted_iota(jnp.int32, (count, LANES), 1) == 0
    mark = jnp.where(first, DEAD, 0.0).astype(jnp.bfloat16)
    blank = jnp.where(
        lax.broadcasted_iota(jnp.int32, (LANES, LANES), 1) == 0, DEAD, 0.0
    )
    pl.semaphore_wait(barrier, bits)
    tell(0)
    last = groups // batch - 1
    order = sorted(range(groups // batch), key=lambda g: (g == last, -g))
    for g in order:
        rows = pl.ds(g * LANES, LANES)
        hit = lax.broadcasted_iota(jnp.int32, (LANES, count), 0) + g * LANES == slot_row
        place = jnp.where(hit, 1.0, 0.0).astype(jnp.bfloat16)
        packed = jnp.dot(place, unit[...], preferred_element_type=jnp.float32)
        used = jnp.dot(place, mark, preferred_element_type=jnp.float32)
        outgoing[rows, :] = packed.astype(jnp.bfloat16)
        outgoing[rows, 0:LANES] = (packed[:, 0:LANES] + (blank - used)).astype(jnp.bfloat16)
        for k in range(max(1, g * batch), (g + 1) * batch):
            if k.bit_count() == 1:
                send(k).start()
    for n in range(1, bits + 1):
        if n > 1:
            hear(n - 2)
            if n < bits:
                tell(n - 1)
        for k in reversed(range(1, groups)):
            if k.bit_count() == n and n > 1:
                send(k).start()
    arrived[0:block, :] = outgoing[0:block, :]
    best[0] = jnp.full((1, total), -1.0, jnp.float32)

    rank_col = jnp.sum(
        jnp.where(same & (col_id < row_id), 1, 0), axis=1, keepdims=True
    )
    slot_col = slot_of(cluster_col, rank_col)
    peer_col = slot_col // block
    chosen = lax.broadcasted_iota(jnp.int32, (count, LANES), 1) == slot_col % LANES

    def scores(one, two):
        left, right = arrived[one[0] : one[1], :], arrived[two[0] : two[1], :]
        gram = lax.dot_general(
            left, right, (((1,), (1,)), ((), ())), preferred_element_type=jnp.float32
        )
        dead = left[:, 0:1].astype(jnp.float32) > 2.0
        this = lax.broadcasted_iota(jnp.int32, gram.shape, 0) + one[0]
        other = lax.broadcasted_iota(jnp.int32, gram.shape, 1) + two[0]
        keep = (((this ^ other) & most) == 0) & (this != other) & jnp.logical_not(dead)
        return jnp.max(jnp.where(keep, gram, -1.0), axis=0, keepdims=True)

    for g in range(groups // batch):
        low, high = g * LANES, (g + 1) * LANES
        for k in range(max(1, g * batch), (g + 1) * batch):
            send(k).wait_recv()
        best[0, :, 0:high] = jnp.maximum(
            best[0, :, 0:high], scores((low, high), (0, high))
        )
        if g:
            best[0, :, low:high] = jnp.maximum(
                best[0, :, low:high], scores((0, low), (low, high))
            )

    def back(k):
        return pltpu.make_async_remote_copy(
            src_ref=best.at[:, :, pl.ds(k // batch * LANES, LANES)],
            dst_ref=returned.at[pl.ds(k, 1)],
            send_sem=back_send_sem.at[k],
            recv_sem=back_recv_sem.at[k],
            device_id={"clu": me ^ k},
            device_id_type=pl.DeviceIdType.MESH,
        )

    for k in range(groups - 1, 0, -1):
        back(k).start()
    returned[0] = best[0, :, 0:LANES]
    for k in range(1, groups):
        send(k).wait_send()
    picked = jnp.broadcast_to(returned[0], (count, LANES))
    for k in range(1, groups):
        back(k).wait_recv()
        picked = jnp.where(peer_col == k, returned[k], picked)
    for k in range(1, groups):
        back(k).wait_send()
    result = jnp.sum(jnp.where(chosen, picked, 0.0), axis=1, keepdims=True)
    result = jnp.sum(jnp.where(row_id == col_id, result, 0.0), axis=0, keepdims=True)
    out_ref[...] = result.reshape(out_ref.shape)


def kernel_shards(embeddings, assignment):
    groups = lax.axis_size("clu")
    count, width = embeddings.shape
    most = 2 * count // (CLU_DEV * groups)
    total = CLU_DEV * groups * most
    return pl.pallas_call(
        functools.partial(exchange_kernel, groups, most),
        out_shape=jax.ShapeDtypeStruct((count,), jnp.float32),
        in_specs=[
            pl.BlockSpec(memory_space=pl.ANY),
            pl.BlockSpec(memory_space=pltpu.VMEM),
        ],
        out_specs=pl.BlockSpec(memory_space=pltpu.VMEM),
        scratch_shapes=[
            pltpu.VMEM((count, width), jnp.bfloat16),
            pltpu.VMEM((total, width), jnp.bfloat16),
            pltpu.VMEM((total, width), jnp.bfloat16),
            pltpu.VMEM((1, 1, total), jnp.float32),
            pltpu.VMEM((groups, 1, LANES), jnp.float32),
            pltpu.SemaphoreType.DMA((4,)),
            pltpu.SemaphoreType.DMA((groups,)),
            pltpu.SemaphoreType.DMA((groups,)),
            pltpu.SemaphoreType.DMA((groups,)),
            pltpu.SemaphoreType.DMA((groups,)),
            pltpu.SemaphoreType.REGULAR((groups.bit_length(), groups.bit_length())),
        ],
        compiler_params=pltpu.CompilerParams(collective_id=0, has_side_effects=True),
    )(embeddings, assignment.reshape(1, count))


def slot_index(cluster, groups, most):
    count = cluster.shape[0]
    order = jnp.argsort(cluster, stable=True)
    ranked = cluster[order]
    first = jnp.searchsorted(ranked, ranked, side="left")
    rank_sorted = jnp.arange(count, dtype=jnp.int32) - first
    rank = jnp.zeros((count,), jnp.int32).at[order].set(rank_sorted)
    local = cluster % CLU_DEV
    owner = cluster // CLU_DEV
    return (local * groups + owner) * most + rank


def cluster_scores(pieces):
    rows, flags = pieces
    items = rows.shape[0]
    width = rows.shape[1] * rows.shape[2]
    rows = rows.reshape(items, width, rows.shape[3])
    flags = flags.reshape(items, width)
    offsets = jnp.arange(width, dtype=jnp.int32)
    distinct = offsets[:, None] != offsets[None, :]

    def single(pair):
        block, marks = pair
        gram = lax.dot_general(
            block, block, (((1,), (1,)), ((), ())), preferred_element_type=jnp.float32
        )
        keep = distinct & (marks > 0)[None, :]
        best = jnp.max(jnp.where(keep, gram, jnp.float32(-2.0)), axis=1)
        return jnp.maximum(best, jnp.float32(-1.0))

    best = lax.map(single, (rows, flags))
    return best.reshape(items, 1, width)


def general_shards(embeddings, assignment):
    groups = lax.axis_size("clu")
    count = embeddings.shape[0]
    width = embeddings.shape[1]
    most = 2 * count // (CLU_DEV * groups)
    unit = normalize(embeddings)
    cluster = assignment[:, 0]
    slot = slot_index(cluster, groups, most)
    total = CLU_DEV * groups * most
    outgoing = jnp.zeros((total, width), jnp.bfloat16).at[slot].set(unit)
    marks = jnp.zeros((total,), jnp.bfloat16).at[slot].set(jnp.ones((count,), jnp.bfloat16))
    outgoing = outgoing.reshape(CLU_DEV, groups, most, width)
    marks = marks.reshape(CLU_DEV, groups, most)
    arrived = (
        lax.all_to_all(outgoing, "clu", split_axis=1, concat_axis=2, tiled=True),
        lax.all_to_all(marks, "clu", split_axis=1, concat_axis=2, tiled=True),
    )
    best = cluster_scores(arrived)
    returned = lax.all_to_all(best, "clu", split_axis=2, concat_axis=1, tiled=True)
    return returned.reshape(total)[slot]


def shards(embeddings, assignment):
    groups = lax.axis_size("clu")
    count = embeddings.shape[0]
    most = 2 * count // (CLU_DEV * groups)
    block = CLU_DEV * most
    power = groups & (groups - 1) == 0 and most & (most - 1) == 0
    if power and block % 16 == 0 and LANES % block == 0 and (groups * block) % LANES == 0:
        return kernel_shards(embeddings, assignment)
    return general_shards(embeddings, assignment)


def solution(mesh):
    in_specs = (P(("lang", "clu"), None), P(("lang", "clu"), None))
    out_specs = P(("lang", "clu"))
    return jax.shard_map(shards, mesh=mesh, in_specs=in_specs, out_specs=out_specs, check_vma=False)
```

profile of v0, /device:TPU:0, one launch (start us, length us, event | category | flops | bytes accessed | tf_op | source)
XLA Modules:
  0.0 36.6 jit_solution(4162963329317231333)
XLA Ops:
  0.0 35.4 %shard_map.28 = f32[256]{0:T(256)} custom-call(bf16[256,1024]{1,0:T(8,128)(2,1)} %emb_ref.1, s32[1,256]{1,0:T(1,128)} %bitcast.1), custom_call_target="tpu_custom_call" | custom-call | tf_op jit(solution)/shard_map/pallas_call | solution.py:182
  35.4 1.2 %copy.4 = f32[256]{0:T(256)} copy(f32[256]{0:T(256)} %shard_map.28) | data formatting | bytes 2048
where the time goes:
time: 36.8 us; the launch traced here: 36.6 us
  Pallas kernels  35.4 us (96%)
  local copies, waits for them, and re-layouts  1.24 us (3%)
    pallas_call x1, Pallas kernels, kernel_shards(): pl.pallas_call(functools.partial(exchange_kernel, groups, most), out_shap...  35.4 us
    unnamed x1, local copies, waits for them, and re-layouts  1.24 us

commit v1 on v0

v1 whole, which is shorter than its diff:
```python
import functools

import jax
import jax.numpy as jnp
from jax import lax
from jax.experimental import pallas as pl
from jax.experimental.pallas import tpu as pltpu
from jax.sharding import PartitionSpec as P

CLU_DEV = 2
LANES = 128
EPS = 1e-06
DEAD = 16.0
ALIVE = 8.0
LOWEST = -1e30
SIDE = 2


def normalize(embeddings):
    values = embeddings.astype(jnp.float32)
    scale = lax.rsqrt(jnp.sum(values * values, axis=-1, keepdims=True) + EPS)
    return (values * scale).astype(jnp.bfloat16)


def exchange_kernel(
    groups, most, emb_ref, cluster_ref, out_ref,
    raw, cluster_in, outgoing, arrived, fence, best, result, returned,
    load_sem, cluster_sem, send_sem, recv_sem, back_send_sem, back_recv_sem, ready,
):
    count, width = raw.shape
    block = CLU_DEV * most
    total = groups * block
    batch = LANES // block
    parts = groups // batch
    half, quarter = groups // 2, groups // 4
    me = lax.axis_index("clu")
    inner = ((me // half) ^ (me // quarter)) & 1
    outer = 1 - inner

    barrier = pltpu.get_barrier_semaphore()
    near = [k for k in range(1, groups) if k & SIDE == 0] + [SIDE]
    for k in near:
        pl.semaphore_signal(
            barrier, inc=1, device_id={"clu": me ^ k},
            device_id_type=pl.DeviceIdType.MESH,
        )
    load_cluster = pltpu.make_async_copy(cluster_ref, cluster_in, cluster_sem)
    load_cluster.start()
    load = pltpu.make_async_copy(emb_ref, raw, load_sem)
    load.start()

    def sent_to(p):
        return p if p < half else p ^ (quarter * outer)

    def landed_from(p):
        return p if p < half else p ^ SIDE

    def piece_of(p):
        if p < total // block - batch:
            return p // batch
        return parts - 1 + (p - (groups - batch)) // (batch // 2)

    def send(p):
        k = sent_to(p)
        peer = me ^ k
        if p < half:
            place, sem = p, piece_of(p)
        else:
            low, top = (p ^ SIDE) % quarter, (p // quarter % 2) ^ outer
            place = half + quarter * top + low
            sem = jnp.where(top == 1, piece_of(half + quarter + low), piece_of(half + low))
        return pltpu.make_async_remote_copy(
            src_ref=outgoing.at[pl.ds(p * block, block)],
            dst_ref=arrived.at[pl.ds(pl.multiple_of(place * block, block), block)],
            send_sem=send_sem,
            recv_sem=recv_sem.at[sem],
            device_id={"clu": peer},
            device_id_type=pl.DeviceIdType.MESH,
        )

    def receive(start, stop):
        rows = pl.ds(start * block, (stop - start) * block)
        return pltpu.make_async_remote_copy(
            src_ref=outgoing.at[rows],
            dst_ref=arrived.at[rows],
            send_sem=send_sem,
            recv_sem=recv_sem.at[piece_of(start)],
            device_id={"clu": me ^ SIDE},
            device_id_type=pl.DeviceIdType.MESH,
        )

    def peer_of(cluster):
        return (cluster // CLU_DEV) ^ me

    def slot_of(cluster, rank):
        peer = peer_of(cluster)
        peer = jnp.where(peer >= half, peer ^ (quarter * outer), peer)
        return peer * block + (cluster % CLU_DEV) * most + rank

    row_id = lax.broadcasted_iota(jnp.int32, (count, count), 0)
    col_id = lax.broadcasted_iota(jnp.int32, (count, count), 1)
    first = lax.broadcasted_iota(jnp.int32, (count, LANES), 1) == 0
    mark = jnp.where(first, DEAD, 0.0).astype(jnp.bfloat16)
    blank = jnp.where(
        lax.broadcasted_iota(jnp.int32, (LANES, LANES), 1) == 0, DEAD, 0.0
    )
    load_cluster.wait()
    cluster_row = cluster_in[...]
    spread = jnp.broadcast_to(cluster_row, (count, count))
    cluster_col = jnp.sum(
        jnp.where(row_id == col_id, spread, 0), axis=1, keepdims=True
    )
    same = cluster_col == spread
    rank_row = jnp.sum(
        jnp.where(same & (row_id < col_id), 1, 0), axis=0, keepdims=True
    )
    slot_row = jnp.broadcast_to(slot_of(cluster_row, rank_row), (LANES, count))

    def pack(g):
        rows = pl.ds(g * LANES, LANES)
        hit = lax.broadcasted_iota(jnp.int32, (LANES, count), 0) + g * LANES == slot_row
        place = jnp.where(hit, 1.0, 0.0).astype(jnp.bfloat16)
        packed = jnp.dot(place, raw[...], preferred_element_type=jnp.float32)
        used = jnp.dot(place, mark, preferred_element_type=jnp.float32)
        outgoing[rows, LANES:width] = packed[:, LANES:width].astype(jnp.bfloat16)
        outgoing[rows, 0:LANES] = (packed[:, 0:LANES] + (blank - used)).astype(jnp.bfloat16)

    def members(g, side):
        span = range(max(1, g * batch), (g + 1) * batch)
        return [p for p in span if (p & SIDE != 0) == side]

    far = parts // 2
    load.wait()
    pack(far)
    pl.semaphore_wait(barrier, len(near))
    pl.semaphore_signal(
        ready, inc=1, device_id={"clu": me ^ SIDE},
        device_id_type=pl.DeviceIdType.MESH,
    )

    @pl.when(inner == 1)
    def _():
        for p in members(far, False):
            send(p).start()

    for g in range(far - 1, 0, -1):
        pack(g)

    @pl.when(outer == 1)
    def _():
        for g in range(far - 1, 0, -1):
            for p in members(g, False):
                send(p).start()
        for p in members(far, False):
            send(p).start()

    pl.semaphore_wait(ready, 1)

    @pl.when(inner == 1)
    def _():
        for p in members(far, True):
            send(p).start()

    @pl.when(outer == 1)
    def _():
        for g in range(far - 1, 0, -1):
            for p in members(g, True):
                send(p).start()
        for p in members(far, True):
            send(p).start()

    raw[...] = normalize(raw[...])
    pack(0)
    for p in members(0, True) + members(0, False):
        send(p).start()
    for g in range(far + 1, parts):
        pack(g)
        for p in members(g, True) + members(g, False):
            send(p).start()
    arrived[0:block, :] = outgoing[0:block, :]

    rank_col = jnp.sum(
        jnp.where(same & (col_id < row_id), 1, 0), axis=1, keepdims=True
    )
    peer_col = peer_of(cluster_col)
    lane_peer = jnp.where(peer_col >= half, peer_col ^ SIDE, peer_col)
    lane_col = lane_peer % batch * block + cluster_col % CLU_DEV * most + rank_col
    chosen = lax.broadcasted_iota(jnp.int32, (count, LANES), 1) == lane_col
    best[...] = jnp.full((total, LANES), -1.0, jnp.float32)

    def score(start, stop):
        low, high = start * block, stop * block
        wide = high - low
        lead = arrived[low:high, 0:LANES].astype(jnp.float32)
        lane = lax.broadcasted_iota(jnp.int32, (wide, LANES), 1)
        row = lax.broadcasted_iota(jnp.int32, (wide, LANES), 0)
        void = jnp.where((lane == 0) & (lead > ALIVE), 1.0, 0.0).astype(jnp.bfloat16)
        ones = jnp.full((LANES, LANES), 1.0, jnp.bfloat16)
        void_col = jnp.dot(void, ones, preferred_element_type=jnp.float32)
        void_row = lax.dot_general(
            ones[0:16], void, (((1,), (1,)), ((), ())), preferred_element_type=jnp.float32
        )[0:1]
        apart = ((row ^ lane) & most) != 0
        fence[low:high, :] = jnp.where(apart | (void_col > 0.5), LOWEST, 0.0)

        if batch <= start < half:
            arrived[low:high, :] = normalize(arrived[low:high, :])
        elif start >= half:
            @pl.when(outer == 1)
            def _():
                arrived[low:high, :] = normalize(arrived[low:high, :])

        gram = lax.dot_general(
            arrived[0:high, :], arrived[low:high, :], (((1,), (1,)), ((), ())),
            preferred_element_type=jnp.float32,
        )
        gram = gram + fence[0:high, 0:wide]
        self_row = lax.broadcasted_iota(jnp.int32, (wide, wide), 0)
        self_col = lax.broadcasted_iota(jnp.int32, (wide, wide), 1)
        own = jnp.where(self_row == self_col, LOWEST, gram[low:high])
        by_col = jnp.max(own, axis=0, keepdims=True)
        bias = void_row * LOWEST
        best[low:high, 0:wide] = jnp.maximum(best[low:high, 0:wide], own + bias)
        if low:
            old = gram[0:low]
            by_col = jnp.maximum(by_col, jnp.max(old, axis=0, keepdims=True))
            best[0:low, 0:wide] = jnp.maximum(best[0:low, 0:wide], old + bias)
        result[0, :, low:high] = by_col

    mid = groups - batch // 2
    pieces = [(g * batch, (g + 1) * batch) for g in range(parts - 1)]
    pieces += [(groups - batch, mid), (mid, groups)]
    for start, stop in pieces:
        receive(max(start, 1), stop).wait_recv()
        if start == batch:
            @pl.when(inner == 1)
            def _():
                for g in range(far - 1, 0, -1):
                    for p in members(g, True) + members(g, False):
                        send(p).start()
        score(start, stop)
    square = lax.broadcasted_iota(jnp.int32, (LANES, LANES), 0) == (
        lax.broadcasted_iota(jnp.int32, (LANES, LANES), 1)
    )
    for g in range(parts):
        span = slice(g * LANES, (g + 1) * LANES)
        top = jnp.max(best[span, :], axis=1, keepdims=True)
        row = jnp.max(jnp.where(square, top, -1.0), axis=0, keepdims=True)
        result[0, :, span] = jnp.maximum(result[0, :, span], row)

    def back(p):
        k = landed_from(p)
        return pltpu.make_async_remote_copy(
            src_ref=result.at[:, :, pl.ds(p // batch * LANES, LANES)],
            dst_ref=returned.at[pl.ds(k, 1)],
            send_sem=back_send_sem,
            recv_sem=back_recv_sem,
            device_id={"clu": me ^ k},
            device_id_type=pl.DeviceIdType.MESH,
        )

    def home():
        return pltpu.make_async_remote_copy(
            src_ref=returned.at[pl.ds(1, groups - 1)],
            dst_ref=returned.at[pl.ds(1, groups - 1)],
            send_sem=back_send_sem,
            recv_sem=back_recv_sem,
            device_id={"clu": me ^ SIDE},
            device_id_type=pl.DeviceIdType.MESH,
        )

    for p in range(groups - 1, 0, -1):
        back(p).start()
    returned[0] = result[0, :, 0:LANES]
    pltpu.make_async_remote_copy(
        src_ref=outgoing.at[pl.ds(block, total - block)],
        dst_ref=arrived.at[pl.ds(block, total - block)],
        send_sem=send_sem,
        recv_sem=recv_sem.at[0],
        device_id={"clu": me ^ SIDE},
        device_id_type=pl.DeviceIdType.MESH,
    ).wait_send()
    home().wait_recv()
    picked = jnp.broadcast_to(returned[0], (count, LANES))
    for k in range(1, groups):
        picked = jnp.where(peer_col == k, returned[k], picked)
    answer = jnp.sum(jnp.where(chosen, picked, 0.0), axis=1, keepdims=True)
    answer = jnp.sum(jnp.where(row_id == col_id, answer, 0.0), axis=0, keepdims=True)
    out_ref[...] = answer.reshape(out_ref.shape)
    home().wait_send()


def kernel_shards(embeddings, assignment):
    groups = lax.axis_size("clu")
    count, width = embeddings.shape
    most = 2 * count // (CLU_DEV * groups)
    total = CLU_DEV * groups * most
    pieces = total // LANES + 1
    return pl.pallas_call(
        functools.partial(exchange_kernel, groups, most),
        out_shape=pltpu.VMEM((count,), jnp.float32),
        in_specs=[
            pl.BlockSpec(memory_space=pl.ANY),
            pl.BlockSpec(memory_space=pl.ANY),
        ],
        out_specs=pl.BlockSpec(memory_space=pltpu.VMEM),
        scratch_shapes=[
            pltpu.VMEM((count, width), jnp.bfloat16),
            pltpu.VMEM((1, count), jnp.int32),
            pltpu.VMEM((total, width), jnp.bfloat16),
            pltpu.VMEM((total, width), jnp.bfloat16),
            pltpu.VMEM((total, LANES), jnp.float32),
            pltpu.VMEM((total, LANES), jnp.float32),
            pltpu.VMEM((1, 1, total), jnp.float32),
            pltpu.VMEM((groups, 1, LANES), jnp.float32),
            pltpu.SemaphoreType.DMA,
            pltpu.SemaphoreType.DMA,
            pltpu.SemaphoreType.DMA,
            pltpu.SemaphoreType.DMA((pieces,)),
            pltpu.SemaphoreType.DMA,
            pltpu.SemaphoreType.DMA,
            pltpu.SemaphoreType.REGULAR,
        ],
        compiler_params=pltpu.CompilerParams(collective_id=0, has_side_effects=True),
    )(embeddings, assignment.reshape(1, count))


def slot_index(cluster, groups, most):
    count = cluster.shape[0]
    order = jnp.argsort(cluster, stable=True)
    ranked = cluster[order]
    first = jnp.searchsorted(ranked, ranked, side="left")
    rank_sorted = jnp.arange(count, dtype=jnp.int32) - first
    rank = jnp.zeros((count,), jnp.int32).at[order].set(rank_sorted)
    local = cluster % CLU_DEV
    owner = cluster // CLU_DEV
    return (local * groups + owner) * most + rank


def cluster_scores(pieces):
    rows, flags = pieces
    items = rows.shape[0]
    width = rows.shape[1] * rows.shape[2]
    rows = rows.reshape(items, width, rows.shape[3])
    flags = flags.reshape(items, width)
    offsets = jnp.arange(width, dtype=jnp.int32)
    distinct = offsets[:, None] != offsets[None, :]

    def single(pair):
        block, marks = pair
        gram = lax.dot_general(
            block, block, (((1,), (1,)), ((), ())), preferred_element_type=jnp.float32
        )
        keep = distinct & (marks > 0)[None, :]
        best = jnp.max(jnp.where(keep, gram, jnp.float32(-2.0)), axis=1)
        return jnp.maximum(best, jnp.float32(-1.0))

    best = lax.map(single, (rows, flags))
    return best.reshape(items, 1, width)


def general_shards(embeddings, assignment):
    groups = lax.axis_size("clu")
    count = embeddings.shape[0]
    width = embeddings.shape[1]
    most = 2 * count // (CLU_DEV * groups)
    unit = normalize(embeddings)
    cluster = assignment[:, 0]
    slot = slot_index(cluster, groups, most)
    total = CLU_DEV * groups * most
    outgoing = jnp.zeros((total, width), jnp.bfloat16).at[slot].set(unit)
    marks = jnp.zeros((total,), jnp.bfloat16).at[slot].set(jnp.ones((count,), jnp.bfloat16))
    outgoing = outgoing.reshape(CLU_DEV, groups, most, width)
    marks = marks.reshape(CLU_DEV, groups, most)
    arrived = (
        lax.all_to_all(outgoing, "clu", split_axis=1, concat_axis=2, tiled=True),
        lax.all_to_all(marks, "clu", split_axis=1, concat_axis=2, tiled=True),
    )
    best = cluster_scores(arrived)
    returned = lax.all_to_all(best, "clu", split_axis=2, concat_axis=1, tiled=True)
    return returned.reshape(total)[slot]


def shards(embeddings, assignment):
    groups = lax.axis_size("clu")
    count = embeddings.shape[0]
    most = 2 * count // (CLU_DEV * groups)
    block = CLU_DEV * most
    power = groups & (groups - 1) == 0 and most & (most - 1) == 0
    if power and block % 16 == 0 and LANES % block == 0 and groups * block == 4 * LANES:
        return kernel_shards(embeddings, assignment)
    return general_shards(embeddings, assignment)


def solution(mesh):
    in_specs = (P(("lang", "clu"), None), P(("lang", "clu"), None))
    out_specs = P(("lang", "clu"))
    return jax.shard_map(shards, mesh=mesh, in_specs=in_specs, out_specs=out_specs, check_vma=False)
```

time: 36.8 us -> 34.3 us (0.932)
  Pallas kernels: 35.4 us -> 33.6 us
  local copies, waits for them, and re-layouts: 1.24 us -> 0.56 us
    pallas_call x1, Pallas kernels: 35.4 us -> 33.6 us  [kernel_shards(): pl.pallas_call(functools.partial(exchange_kernel, groups, most), out_shap...]
    unnamed x1, local copies, waits for them, and re-layouts: 1.24 us -> 0.56 us
where the time goes in v1:
time: 34.3 us; the launch traced here: 34.2 us
  Pallas kernels  33.6 us (98%)
  local copies, waits for them, and re-layouts  0.56 us (2%)
    pallas_call x1, Pallas kernels, kernel_shards(): pl.pallas_call(functools.partial(exchange_kernel, groups, most), out_shap...  33.6 us

profile of v1, /device:TPU:0, one launch (start us, length us, event | category | flops | bytes accessed | tf_op | source)
XLA Modules:
  0.0 34.2 jit_solution(7572858450788940912)
XLA Ops:
  0.0 33.6 %shard_map.28 = f32[256]{0:T(256)S(1)} custom-call(bf16[256,1024]{1,0:T(8,128)(2,1)} %emb_ref.1, s32[1,256]{1,0:T(1,128)} %bitcast.1), custom_call_target="tpu_custom_call" | custom-call | tf_op jit(solution)/shard_map/pallas_call | solution.py:299
  33.6 0.6 %copy.4 = f32[256]{0:T(256)} copy(f32[256]{0:T(256)S(1)} %shard_map.28) | data formatting | bytes 2048
